TPU v7x, 32 devices: a whole 2x2x4 slice. The times are simulated.
32 devices in a mesh: dp: 8 (over y, x, core), tensor: 4 (over z).
Axes of the slice: x: 2, y: 2, z: 4, core: 2. Of those that a mesh axis runs over, the one named last changes fastest.
Arguments:
- tokens: bfloat16 [32, 256, 1152], P(('dp', 'tensor')), may hold values from -6 to 6
- timesteps: int32 [32], P('dp'), may hold values from 0 to 999
- labels: int32 [32], P('dp'), may hold values from 0 to 999
- item_counts: int32 [8], P('dp'), may hold values from 1 to 4
- cotangent: bfloat16 [32, 256, 1152], P(('dp', 'tensor')), may hold values from -6 to 6
- project_weight: bfloat16 [1152, 3, 1152], P(None, None, 'tensor'), may hold values from -0.1875 to 0.1875
- query_gain: bfloat16 [72], replicated, may hold values from 0.099609375 to 1.8984375
- key_gain: bfloat16 [72], replicated, may hold values from 0.099609375 to 1.8984375
- output_weight: bfloat16 [1152, 1152], P('tensor'), may hold values from -0.5 to 0.5
- output_bias: bfloat16 [1152], replicated, may hold values from -3 to 3
- expand_weight: bfloat16 [1152, 2, 3072], P(None, None, 'tensor'), may hold values from -0.1875 to 0.1875
- down_weight: bfloat16 [3072, 1152], P('tensor'), may hold values from -0.15625 to 0.15625
- down_bias: bfloat16 [1152], replicated, may hold values from -3 to 3
- modulate_weight: bfloat16 [1152, 6, 1152], P(None, None, 'tensor'), may hold values from -0.1875 to 0.1875
- modulate_bias: bfloat16 [6, 1152], P(None, 'tensor'), may hold values from -3 to 3
- time_weight: bfloat16 [256, 1152], replicated, may hold values from -0.5 to 0.5
- time_bias: bfloat16 [1152], replicated, may hold values from -3 to 3
- embed_weight: bfloat16 [1152, 1152], replicated, may hold values from -0.25 to 0.25
- embed_bias: bfloat16 [1152], replicated, may hold values from -3 to 3
- class_table: bfloat16 [1000, 1152], replicated, may hold values from -6 to 6
Outputs:
- result: bfloat16 [32, 256, 1152], P(('dp', 'tensor'))
- tokens_grad: bfloat16 [32, 256, 1152], P(('dp', 'tensor'))
- project_grad: float32 [1152, 3, 1152], P('dp', None, 'tensor')
- query_gain_grad: float32 [72], replicated
- key_gain_grad: float32 [72], replicated
- output_weight_grad: float32 [1152, 1152], P('tensor', 'dp')
- output_bias_grad: float32 [1152], replicated
- expand_grad: float32 [1152, 2, 3072], P('dp', None, 'tensor')
- down_grad: float32 [3072, 1152], P('tensor', 'dp')
- down_bias_grad: float32 [1152], replicated
- modulate_grad: float32 [1152, 6, 1152], P('dp', None, 'tensor')
- modulate_bias_grad: float32 [6, 1152], replicated
- time_grad: float32 [256, 1152], P(None, 'dp')
- time_bias_grad: float32 [1152], P('dp')
- embed_grad: float32 [1152, 1152], P('dp')
- embed_bias_grad: float32 [1152], P('dp')
- class_grad: float32 [1000, 1152], P(None, 'dp')
Inputs may be any that keep to these rules, and one draw needn't show every extreme that they name: `item_counts`: entry i counts the real items among the 4 items of index i of dp; they are its first ones.
All inputs are finite; a program needn't handle non-finite values.
Results may differ from a plain program's by a relative error of at most 0.03.
Values may be sent and summed in bfloat16 or wider, within the bound.
A program may use at most 256 MiB of HBM per device.

v0:
```python
import math
import jax
import jax.numpy as jnp
from jax import lax
from jax.sharding import PartitionSpec as P

HD = 72
FREQ = 256
GRID = 16
EPS = 1e-06


def layer_norm(value):
    center = value - jnp.mean(value, axis=-1, keepdims=True)
    inverse = lax.rsqrt(jnp.mean(center * center, axis=-1, keepdims=True) + EPS)
    return (center * inverse, inverse)


def layer_norm_back(normed, inverse, grad):
    return inverse * (
        grad
        - jnp.mean(grad, axis=-1, keepdims=True)
        - normed * jnp.mean(grad * normed, axis=-1, keepdims=True)
    )


def silu_slope(value):
    sigma = jax.nn.sigmoid(value)
    return sigma * (1.0 + value * (1.0 - sigma))


def rotate(value, positions):
    quarter = HD // 4
    rates = 10000.0 ** (-jnp.arange(quarter, dtype=jnp.float32) / quarter)
    places = ((positions // GRID).astype(jnp.float32), (positions % GRID).astype(jnp.float32))
    pieces = []
    for which_half in range(2):
        half_value = value[..., which_half * 2 * quarter : (which_half + 1) * 2 * quarter]
        angle = places[which_half][:, None] * rates[None, :]
        cosine = jnp.cos(angle)[None, :, None, :]
        sine = jnp.sin(angle)[None, :, None, :]
        first = half_value[..., :quarter]
        second = half_value[..., quarter:]
        pieces.append(first * cosine - second * sine)
        pieces.append(second * cosine + first * sine)
    return jnp.concatenate(pieces, axis=-1)


def head_prepare(raw, gain, positions):
    scaled = raw * lax.rsqrt(jnp.mean(raw * raw, axis=-1, keepdims=True) + EPS) * gain
    return rotate(scaled, positions)


def time_features(steps_in):
    half = FREQ // 2
    rates = jnp.exp(-math.log(10000.0) * jnp.arange(half, dtype=jnp.float32) / half)
    angle = steps_in.astype(jnp.float32)[:, None] * rates[None, :]
    return jnp.concatenate([jnp.cos(angle), jnp.sin(angle)], axis=-1)


def shards(
    tokens,
    timesteps,
    labels,
    item_counts,
    cotangent,
    project_weight,
    query_gain,
    key_gain,
    output_weight,
    output_bias,
    expand_weight,
    down_weight,
    down_bias,
    modulate_weight,
    modulate_bias,
    time_weight,
    time_bias,
    embed_weight,
    embed_bias,
    class_table,
):
    local_items, length, width = tokens.shape
    items = timesteps.shape[0]
    slab = modulate_weight.shape[2]
    heads_here = project_weight.shape[2] // HD
    scale = HD ** (-0.5)
    lane = lax.axis_index("tensor")
    first_item = lane * local_items
    live = (first_item + jnp.arange(local_items) < item_counts[0]).astype(jnp.float32)[
        :, None, None
    ]
    time_feat = time_features(timesteps).astype(jnp.bfloat16)
    pre_hidden = jnp.dot(
        time_feat, time_weight, preferred_element_type=jnp.float32
    ) + time_bias.astype(jnp.float32)
    time_hidden = jax.nn.silu(pre_hidden).astype(jnp.bfloat16)
    condition = (
        jnp.dot(time_hidden, embed_weight, preferred_element_type=jnp.float32)
        + embed_bias.astype(jnp.float32)
        + jnp.take(class_table, labels, axis=0).astype(jnp.float32)
    )
    cond_act = jax.nn.silu(condition).astype(jnp.bfloat16)
    modulation_part = (
        jnp.einsum("bd,dke->bke", cond_act, modulate_weight, preferred_element_type=jnp.float32)
        + modulate_bias.astype(jnp.float32)
    ).astype(jnp.bfloat16)
    token_all, modulation = (
        lax.all_gather(tokens, "tensor", axis=0, tiled=True),
        lax.all_gather(modulation_part, "tensor", axis=2, tiled=True),
    )
    modulation = modulation.astype(jnp.float32)
    modulation_local = lax.dynamic_slice_in_dim(modulation, first_item, local_items, 0)
    attend_shift_all = modulation[:, 0][:, None, :]
    attend_scale_all = modulation[:, 1][:, None, :]
    local_parts = [modulation_local[:, which][:, None, :] for which in range(6)]
    _, attend_scale, attend_gate, feed_shift, feed_scale, feed_gate = local_parts
    positions = jnp.arange(length)
    normed_all, _ = layer_norm(token_all.astype(jnp.float32))
    mod_in = (normed_all * (1.0 + attend_scale_all) + attend_shift_all).astype(jnp.bfloat16)
    projected = jnp.einsum(
        "bld,dke->blke", mod_in, project_weight, preferred_element_type=jnp.float32
    )
    split = projected.reshape(items, length, 3, heads_here, HD)
    query_gain_f = query_gain.astype(jnp.float32)
    key_gain_f = key_gain.astype(jnp.float32)
    queries = head_prepare(split[:, :, 0], query_gain_f, positions).astype(jnp.bfloat16)
    keys = head_prepare(split[:, :, 1], key_gain_f, positions).astype(jnp.bfloat16)
    values = split[:, :, 2].astype(jnp.bfloat16)
    scores = (
        jnp.einsum("bqhd,bkhd->bhqk", queries, keys, preferred_element_type=jnp.float32) * scale
    )
    top = jnp.max(scores, axis=-1, keepdims=True)
    logsum = top + jnp.log(jnp.sum(jnp.exp(scores - top), axis=-1, keepdims=True))
    probs = jnp.exp(scores - logsum).astype(jnp.bfloat16)
    mixed = jnp.einsum("bhqk,bkhd->bqhd", probs, values, preferred_element_type=jnp.float32)
    mixed = mixed.reshape(items, length, heads_here * HD).astype(jnp.bfloat16)
    piece = mixed
    attend_branch = lax.psum_scatter(
        jnp.einsum("blh,hd->bld", piece, output_weight, preferred_element_type=jnp.float32).astype(
            jnp.bfloat16
        ),
        "tensor",
        scatter_dimension=0,
        tiled=True,
    ).astype(jnp.float32) + output_bias.astype(jnp.float32)
    token_local = tokens.astype(jnp.float32)
    normed_local, inverse_local = layer_norm(token_local)
    residual = token_local + attend_gate * attend_branch
    normed_two, inverse_two = layer_norm(residual)
    mod_two = (normed_two * (1.0 + feed_scale) + feed_shift).astype(jnp.bfloat16)
    mod_two_all = lax.all_gather(mod_two, "tensor", axis=0, tiled=True)
    gate_up = jnp.einsum(
        "bld,dkf->blkf", mod_two_all, expand_weight, preferred_element_type=jnp.float32
    )
    gate = gate_up[:, :, 0]
    upper = gate_up[:, :, 1]
    hidden = (jax.nn.silu(gate) * upper).astype(jnp.bfloat16)
    piece = hidden
    feed_branch = lax.psum_scatter(
        jnp.einsum("blf,fd->bld", piece, down_weight, preferred_element_type=jnp.float32).astype(
            jnp.bfloat16
        ),
        "tensor",
        scatter_dimension=0,
        tiled=True,
    ).astype(jnp.float32) + down_bias.astype(jnp.float32)
    result = (live * (residual + feed_gate * feed_branch)).astype(jnp.bfloat16)
    out_grad = cotangent.astype(jnp.float32) * live
    branch_grad = (out_grad * feed_gate).astype(jnp.bfloat16)
    down_bias_part = jnp.sum(branch_grad.astype(jnp.float32), axis=(0, 1))
    piece = lax.all_gather(branch_grad, "tensor", axis=0, tiled=True)
    weight_total = jnp.einsum("blf,bld->fd", hidden, piece, preferred_element_type=jnp.float32)
    rows_grad = jnp.einsum("bld,fd->blf", piece, down_weight, preferred_element_type=jnp.float32)
    hidden_total = rows_grad
    down_grad = weight_total
    gate_up_grad = jnp.stack(
        [hidden_total * upper * silu_slope(gate), hidden_total * jax.nn.silu(gate)], axis=2
    ).astype(jnp.bfloat16)
    expand_grad = jnp.einsum(
        "bld,blkf->dkf", mod_two_all, gate_up_grad, preferred_element_type=jnp.float32
    )
    piece = gate_up_grad
    mod_two_grad = lax.psum_scatter(
        jnp.einsum(
            "blkf,dkf->bld", piece, expand_weight, preferred_element_type=jnp.float32
        ).astype(jnp.bfloat16),
        "tensor",
        scatter_dimension=0,
        tiled=True,
    ).astype(jnp.float32)
    residual_grad = out_grad + layer_norm_back(
        normed_two, inverse_two, mod_two_grad * (1.0 + feed_scale)
    )
    attend_grad = (residual_grad * attend_gate).astype(jnp.bfloat16)
    output_bias_part = jnp.sum(attend_grad.astype(jnp.float32), axis=(0, 1))
    piece = lax.all_gather(attend_grad, "tensor", axis=0, tiled=True)
    weight_total = jnp.einsum("blh,bld->hd", mixed, piece, preferred_element_type=jnp.float32)
    rows_grad = jnp.einsum("bld,hd->blh", piece, output_weight, preferred_element_type=jnp.float32)
    output_weight_grad = weight_total
    mixed_grad = rows_grad
    mixed_grad = mixed_grad.reshape(items, length, heads_here, HD).astype(jnp.bfloat16)
    again = jnp.einsum("bqhd,bkhd->bhqk", queries, keys, preferred_element_type=jnp.float32) * scale
    prob_float = jnp.exp(again - logsum)
    prob_low = prob_float.astype(jnp.bfloat16)
    prob_grad = jnp.einsum(
        "bqhd,bkhd->bhqk", mixed_grad, values, preferred_element_type=jnp.float32
    )
    score_grad = (
        prob_float * (prob_grad - jnp.sum(prob_float * prob_grad, axis=-1, keepdims=True))
    ).astype(jnp.bfloat16)
    query_grad = (
        jnp.einsum("bhqk,bkhd->bqhd", score_grad, keys, preferred_element_type=jnp.float32) * scale
    )
    key_grad = (
        jnp.einsum("bhqk,bqhd->bkhd", score_grad, queries, preferred_element_type=jnp.float32)
        * scale
    )
    value_grad = jnp.einsum(
        "bhqk,bqhd->bkhd", prob_low, mixed_grad, preferred_element_type=jnp.float32
    )

    def prepare_here(raw, gain):
        return head_prepare(raw, gain, positions)

    _, query_back = jax.vjp(prepare_here, split[:, :, 0], query_gain_f)
    raw_query_grad, query_gain_part = query_back(query_grad)
    _, key_back = jax.vjp(prepare_here, split[:, :, 1], key_gain_f)
    raw_key_grad, key_gain_part = key_back(key_grad)
    projected_grad = jnp.stack([raw_query_grad, raw_key_grad, value_grad], axis=2)
    projected_grad = projected_grad.reshape(items, length, 3, heads_here * HD).astype(jnp.bfloat16)
    project_grad = jnp.einsum(
        "bld,blke->dke", mod_in, projected_grad, preferred_element_type=jnp.float32
    )
    piece = projected_grad
    mod_in_grad = lax.psum_scatter(
        jnp.einsum(
            "blke,dke->bld", piece, project_weight, preferred_element_type=jnp.float32
        ).astype(jnp.bfloat16),
        "tensor",
        scatter_dimension=0,
        tiled=True,
    ).astype(jnp.float32)
    tokens_grad = (
        residual_grad
        + layer_norm_back(normed_local, inverse_local, mod_in_grad * (1.0 + attend_scale))
    ).astype(jnp.bfloat16)
    modulation_grad_part = jnp.stack(
        [
            jnp.sum(mod_in_grad, axis=1),
            jnp.sum(mod_in_grad * normed_local, axis=1),
            jnp.sum(residual_grad * attend_branch, axis=1),
            jnp.sum(mod_two_grad, axis=1),
            jnp.sum(mod_two_grad * normed_two, axis=1),
            jnp.sum(out_grad * feed_branch, axis=1),
        ],
        axis=1,
    )
    modulation_grad = lax.all_to_all(
        modulation_grad_part, "tensor", split_axis=2, concat_axis=0, tiled=True
    ).astype(jnp.bfloat16)
    modulate_bias_part = jnp.sum(modulation_grad.astype(jnp.float32), axis=0)
    cond_part = jnp.einsum(
        "bke,dke->bd", modulation_grad, modulate_weight, preferred_element_type=jnp.float32
    )
    cond_total = lax.psum(cond_part, "tensor")
    cond_grad = (cond_total * silu_slope(condition)).astype(jnp.bfloat16)
    one_hot = (labels[:, None] == jnp.arange(class_table.shape[0])[None, :]).astype(jnp.bfloat16)
    class_grad = jnp.einsum("bc,bd->cd", one_hot, cond_grad, preferred_element_type=jnp.float32)
    pre_grad = (
        jnp.einsum("be,de->bd", cond_grad, embed_weight, preferred_element_type=jnp.float32)
        * silu_slope(pre_hidden)
    ).astype(jnp.bfloat16)
    bias_wide = lax.dynamic_update_slice_in_dim(
        jnp.zeros((6, width), jnp.float32), modulate_bias_part, lane * slab, 1
    )
    output_bias_grad, down_bias_grad, query_gain_grad, key_gain_grad, modulate_bias_grad = lax.psum(
        (output_bias_part, down_bias_part, query_gain_part, key_gain_part, bias_wide),
        ("dp", "tensor"),
    )
    modulate_local = jnp.einsum(
        "bd,bke->dke", cond_act, modulation_grad, preferred_element_type=jnp.float32
    )
    embed_local = jnp.einsum(
        "bd,be->de", time_hidden, cond_grad, preferred_element_type=jnp.float32
    )
    embed_bias_local = jnp.sum(cond_grad.astype(jnp.float32), axis=0)
    time_local = jnp.einsum("bf,bd->fd", time_feat, pre_grad, preferred_element_type=jnp.float32)
    time_bias_local = jnp.sum(pre_grad.astype(jnp.float32), axis=0)
    (
        project_grad,
        output_weight_grad,
        expand_grad,
        down_grad,
        class_grad,
        modulate_grad,
        time_grad,
        time_bias_grad,
        embed_grad,
        embed_bias_grad,
    ) = (
        lax.psum_scatter(project_grad, "dp", scatter_dimension=0, tiled=True),
        lax.psum_scatter(output_weight_grad, "dp", scatter_dimension=1, tiled=True),
        lax.psum_scatter(expand_grad, "dp", scatter_dimension=0, tiled=True),
        lax.psum_scatter(down_grad, "dp", scatter_dimension=1, tiled=True),
        lax.psum_scatter(class_grad, "dp", scatter_dimension=1, tiled=True),
        lax.psum_scatter(modulate_local, "dp", scatter_dimension=0, tiled=True),
        lax.psum_scatter(time_local, "dp", scatter_dimension=1, tiled=True),
        lax.psum_scatter(time_bias_local, "dp", scatter_dimension=0, tiled=True),
        lax.psum_scatter(embed_local, "dp", scatter_dimension=0, tiled=True),
        lax.psum_scatter(embed_bias_local, "dp", scatter_dimension=0, tiled=True),
    )
    return (
        result,
        tokens_grad,
        project_grad,
        query_gain_grad,
        key_gain_grad,
        output_weight_grad,
        output_bias_grad,
        expand_grad,
        down_grad,
        down_bias_grad,
        modulate_grad,
        modulate_bias_grad,
        time_grad,
        time_bias_grad,
        embed_grad,
        embed_bias_grad,
        class_grad,
    )


def solution(mesh):
    return jax.shard_map(
        shards,
        mesh=mesh,
        in_specs=(
            P(("dp", "tensor"), None, None),
            P("dp"),
            P("dp"),
            P("dp"),
            P(("dp", "tensor"), None, None),
            P(None, None, "tensor"),
            P(),
            P(),
            P("tensor", None),
            P(),
            P(None, None, "tensor"),
            P("tensor", None),
            P(),
            P(None, None, "tensor"),
            P(None, "tensor"),
            P(),
            P(),
            P(),
            P(),
            P(),
        ),
        out_specs=(
            P(("dp", "tensor"), None, None),
            P(("dp", "tensor"), None, None),
            P("dp", None, "tensor"),
            P(),
            P(),
            P("tensor", "dp"),
            P(),
            P("dp", None, "tensor"),
            P("tensor", "dp"),
            P(),
            P("dp", None, "tensor"),
            P(),
            P(None, "dp"),
            P("dp"),
            P("dp", None),
            P("dp"),
            P(None, "dp"),
        ),
        check_vma=False,
    )
```

profile of v0, /device:TPU:0, one launch (start us, length us, event | category | flops | bytes accessed | tf_op | source)
XLA Modules:
  0.0 962.4 jit_solution(16076023338928004156)
XLA Ops:
  23.1 44.6 %all_gather.15 = bf16[4,6,1152]{1,0,2:T(4,128)(2,1)} all-gather(bf16[4,6,288]{1,0,2:T(4,128)(2,1)S(1)} %copy.105), channel_id=1, replica_groups=mesh['dp'=8,'tensor'=4] {'tensor'}, dimensions={2}, use_global_device_ids=true | all-gather | bytes 69120 | tf_op jit(solution)/shard_map/all_gather | solution.py:110
  70.1 11.2 %all-gather.5.cloned.1.call-done = bf16[4,256,1152]{2,1,0:T(8,128)(2,1)} async-done(((bf16[1,256,1152]{2,1,0:T(8,128)(2,1)}), bf16[4,256,1152]{2,1,0:T(8,128)(2,1)}) %all-gather.5.cloned.1.call-update) | async-done | bytes 2359312 | tf_op jit(solution)/shard_map/all_gather | solution.py:109
  101.6 43.7 %reduce-scatter.13.cloned.1.call-done = bf16[1,256,1152]{2,1,0:T(8,128)(2,1)} async-done(((bf16[4,256,1152]{2,1,0:T(8,128)(2,1)}), bf16[1,256,1152]{2,1,0:T(8,128)(2,1)}) %reduce-scatter.13.cloned.1.call-update) | async-done | bytes 589840 | tf_op jit(solution)/shard_map/reduce_scatter | solution.py:139
  153.1 46.1 %all-gather.7.cloned.1.call-done = bf16[4,256,1152]{2,1,0:T(8,128)(2,1)} async-done(((bf16[1,256,1152]{2,1,0:T(8,128)(2,1)}), bf16[4,256,1152]{2,1,0:T(8,128)(2,1)}) %all-gather.7.cloned.1.call-update) | async-done | bytes 2359312 | tf_op jit(solution)/shard_map/all_gather | solution.py:152
  199.2 9.6 fusion.7
  208.8 41.2 %all-gather.9.cloned.1.call-done = bf16[4,256,1152]{2,1,0:T(8,128)(2,1)} async-done(((bf16[1,256,1152]{2,1,0:T(8,128)(2,1)}), bf16[4,256,1152]{2,1,0:T(8,128)(2,1)}) %all-gather.9.cloned.1.call-update) | async-done | bytes 2359312 | tf_op jit(solution)/shard_map/all_gather | solution.py:172
  250.0 8.4 fusion.30
  272.8 39.4 %reduce-scatter.17.cloned.1.call-done = bf16[1,256,1152]{2,1,0:T(8,128)(2,1)} async-done(((bf16[4,256,1152]{2,1,0:T(8,128)(2,1)}), bf16[1,256,1152]{2,1,0:T(8,128)(2,1)}) %reduce-scatter.17.cloned.1.call-update) | async-done | bytes 589840 | tf_op jit(solution)/shard_map/reduce_scatter | solution.py:184
  316.7 44.8 %reduce-scatter.15.cloned.1.call-done = bf16[1,256,1152]{2,1,0:T(8,128)(2,1)} async-done(((bf16[4,256,1152]{2,1,0:T(8,128)(2,1)}), bf16[1,256,1152]{2,1,0:T(8,128)(2,1)}) %reduce-scatter.15.cloned.1.call-update) | async-done | bytes 589840 | tf_op jit(solution)/shard_map/reduce_scatter | solution.py:160
  368.5 49.5 %all-gather.11.cloned.1.call-done = bf16[4,256,1152]{2,1,0:T(8,128)(2,1)} async-done(((bf16[1,256,1152]{2,1,0:T(8,128)(2,1)}), bf16[4,256,1152]{2,1,0:T(8,128)(2,1)}) %all-gather.11.cloned.1.call-update) | async-done | bytes 2359312 | tf_op jit(solution)/shard_map/all_gather | solution.py:197
  439.6 9.4 convolution_bitcast_fusion
  460.4 8.2 convolution_bitcast_fusion.1
  469.4 16.4 %reduce-scatter.19.cloned.1.call-done = bf16[1,256,1152]{2,1,0:T(8,128)(2,1)} async-done(((bf16[4,256,1152]{2,1,0:T(8,128)(2,1)}), bf16[1,256,1152]{2,1,0:T(8,128)(2,1)}) %reduce-scatter.19.cloned.1.call-update) | async-done | bytes 589840 | tf_op jit(solution)/shard_map/reduce_scatter | solution.py:236
  498.6 8.8 all_to_all.4
  513.0 16.3 %psum.47 = f32[4,1152]{1,0:T(4,128)S(1)} all-reduce(f32[4,1152]{1,0:T(4,128)S(1)} %convolution_bitcast_fusion.4), channel_id=1, replica_groups=mesh['dp'=8,'tensor'=4] {'tensor'}, use_global_device_ids=true, to_apply=%region_42.43 | all-reduce | flops 4608 | bytes 36864 | tf_op jit(solution)/shard_map/psum | solution.py:266
  545.7 8.4 reduce-scatter.25.cloned.1.call-done
  558.4 22.9 %all-reduce.15 = (f32[1152]{0:T(1024)S(1)}, f32[1152]{0:T(1024)S(1)}) all-reduce(f32[1152]{0:T(1024)S(1)} %get-tuple-element.164, f32[1152]{0:T(1024)S(1)} %get-tuple-element.110), channel_id=12, replica_groups=mesh['dp'=8,'tensor'=4] {'dp'}, use_global_device_ids=true, to_apply=%region_45.46.clone | all-reduce | flops 2304 | bytes 18432
  583.0 40.9 %all-reduce.14 = (f32[72]{0:T(128)}, f32[72]{0:T(128)}, f32[1152]{0:T(1024)}, f32[1152]{0:T(1024)}, f32[6,1152]{1,0:T(8,128)}) all-reduce(f32[72]{0:T(128)S(1)} %copy-done.80, f32[72]{0:T(128)S(1)} %copy-done.79, f32[1152]{0:T(1024)S(1)} %copy-done.51, f32[1152]{0:T(1024)S(1)} %copy-done.50, ...), channel_id=1, replica_groups=mesh['dp'=8,'tensor'=4] {'dp','tensor'}, use_global_device_ids=true, to_apply=%region_23.24 | all-reduce | flops 9360 | bytes 74880 | tf_op jit(solution)/shard_map/psum | solution.py:277
  623.8 25.9 %reduce-scatter.23.cloned.1.call-done = f32[288,144]{0,1:T(8,128)} async-done(((f32[288,1152]{0,1:T(8,128)}), f32[288,144]{0,1:T(8,128)}) %reduce-scatter.23.cloned.1.call-update) | async-done | bytes 165904 | tf_op jit(solution)/shard_map/reduce_scatter | solution.py:303
  649.8 60.7 %reduce-scatter.21.cloned.1.call-done = f32[144,3,288]{2,0,1:T(8,128)} async-done(((f32[1152,3,288]{2,0,1:T(8,128)}), f32[144,3,288]{2,0,1:T(8,128)}) %reduce-scatter.21.cloned.1.call-update) | async-done | bytes 497680 | tf_op jit(solution)/shard_map/reduce_scatter | solution.py:302
  710.4 40.5 %reduce-scatter.31.cloned.1.call-done = f32[256,144]{0,1:T(8,128)} async-done(((f32[256,1152]{0,1:T(8,128)}), f32[256,144]{0,1:T(8,128)}) %reduce-scatter.31.cloned.1.call-update) | async-done | bytes 147472 | tf_op jit(solution)/shard_map/reduce_scatter | solution.py:308
  750.9 57.7 %reduce-scatter.35.cloned.1.call-done = f32[1000,144]{0,1:T(8,128)} async-done(((f32[1000,1152]{0,1:T(8,128)}), f32[1000,144]{0,1:T(8,128)}) %reduce-scatter.35.cloned.1.call-update) | async-done | bytes 576016 | tf_op jit(solution)/shard_map/reduce_scatter | solution.py:306
  808.6 60.7 %reduce-scatter.33.cloned.1.call-done = f32[144,1152]{1,0:T(8,128)} async-done(((f32[1152,1152]{1,0:T(8,128)}), f32[144,1152]{1,0:T(8,128)}) %reduce-scatter.33.cloned.1.call-update) | async-done | bytes 663568 | tf_op jit(solution)/shard_map/reduce_scatter | solution.py:310
  869.4 86.3 %reduce-scatter.29.cloned.1.call-done = f32[144,6,288]{2,0,1:T(8,128)} async-done(((f32[1152,6,288]{2,0,1:T(8,128)}), f32[144,6,288]{2,0,1:T(8,128)}) %reduce-scatter.29.cloned.1.call-update) | async-done | bytes 995344 | tf_op jit(solution)/shard_map/reduce_scatter | solution.py:307
  (322 shorter events, 144.3 us)
Async XLA Ops:
  7.2 74.1 %all-gather.5.cloned.1.call-start = ((), (), s32[]{:S(2)}) async-start(), calls=%async_computation.13 | async-start | bytes 2949120 | tf_op jit(solution)/shard_map/all_gather | solution.py:109
  7.9 137.3 %reduce-scatter.13.cloned.1.call-start = ((), (), s32[]{:S(2)}) async-start(), calls=%async_computation.14 | async-start | bytes 2949120 | tf_op jit(solution)/shard_map/reduce_scatter | solution.py:139
  8.7 79.7 %copy-start.70 = (f32[72]{0:T(128)}, f32[72]{0:T(128)S(1)}, u32[]{:S(2)}) copy-start(f32[72]{0:T(128)S(1)} %convert_element_type.252) | copy-start | bytes 868
  9.3 79.3 %copy-start.72 = (f32[72]{0:T(128)}, f32[72]{0:T(128)S(1)}, u32[]{:S(2)}) copy-start(f32[72]{0:T(128)S(1)} %convert_element_type.255) | copy-start | bytes 868
  98.6 46.7 %copy-start.3 = (bf16[1,256,1152]{2,1,0:T(8,128)(2,1)S(1)}, bf16[1,256,1152]{2,1,0:T(8,128)(2,1)}, u32[]{:S(2)}) copy-start(bf16[1,256,1152]{2,1,0:T(8,128)(2,1)} %param.20) | copy-start | bytes 1769476
  98.6 100.6 %all-gather.7.cloned.1.call-start = ((), (), s32[]{:S(2)}) async-start(), calls=%async_computation.15 | async-start | bytes 2949120 | tf_op jit(solution)/shard_map/all_gather | solution.py:152
  149.7 100.3 %all-gather.9.cloned.1.call-start = ((), (), s32[]{:S(2)}) async-start(), calls=%async_computation.17 | async-start | bytes 2949120 | tf_op jit(solution)/shard_map/all_gather | solution.py:172
  153.1 159.1 %reduce-scatter.17.cloned.1.call-start = ((), (), s32[]{:S(2)}) async-start(), calls=%async_computation.18 | async-start | bytes 2949120 | tf_op jit(solution)/shard_map/reduce_scatter | solution.py:184
  265.6 95.9 %reduce-scatter.15.cloned.1.call-start = ((), (), s32[]{:S(2)}) async-start(), calls=%async_computation.16 | async-start | bytes 2949120 | tf_op jit(solution)/shard_map/reduce_scatter | solution.py:160
  271.2 146.7 %all-gather.11.cloned.1.call-start = ((), (), s32[]{:S(2)}) async-start(), calls=%async_computation.19 | async-start | bytes 2949120 | tf_op jit(solution)/shard_map/all_gather | solution.py:197
  368.5 117.3 %reduce-scatter.19.cloned.1.call-start = ((), (), s32[]{:S(2)}) async-start(), calls=%async_computation.20 | async-start | bytes 2949120 | tf_op jit(solution)/shard_map/reduce_scatter | solution.py:236
  439.2 115.0 %reduce-scatter.25.cloned.1.call-start = ((), (), s32[]{:S(2)}) async-start(), calls=%async_computation.23 | async-start | bytes 7962624 | tf_op jit(solution)/shard_map/reduce_scatter | solution.py:304
  449.1 174.8 %reduce-scatter.27.cloned.1.call-start = ((), (), s32[]{:S(2)}) async-start(), calls=%async_computation.24 | async-start | bytes 3981312 | tf_op jit(solution)/shard_map/reduce_scatter | solution.py:305
  455.1 194.7 %reduce-scatter.23.cloned.1.call-start = ((), (), s32[]{:S(2)}) async-start(), calls=%async_computation.22 | async-start | bytes 1990656 | tf_op jit(solution)/shard_map/reduce_scatter | solution.py:303
  459.7 250.7 %reduce-scatter.21.cloned.1.call-start = ((), (), s32[]{:S(2)}) async-start(), calls=%async_computation.21 | async-start | bytes 5971968 | tf_op jit(solution)/shard_map/reduce_scatter | solution.py:302
  468.7 282.3 %reduce-scatter.31.cloned.1.call-start = ((), (), s32[]{:S(2)}) async-start(), calls=%async_computation.26 | async-start | bytes 1327104 | tf_op jit(solution)/shard_map/reduce_scatter | solution.py:308
  510.2 19.1 %copy-start.38 = (f32[4,1152]{1,0:T(4,128)S(1)}, f32[4,1152]{1,0:T(4,128)}, u32[]{:S(2)}) copy-start(f32[4,1152]{1,0:T(4,128)} %copy-done.37) | copy-start | bytes 55300
  531.6 277.0 %reduce-scatter.35.cloned.1.call-start = ((), (), s32[]{:S(2)}) async-start(), calls=%async_computation.28 | async-start | bytes 5308416 | tf_op jit(solution)/shard_map/reduce_scatter | solution.py:306
  534.7 334.7 %reduce-scatter.33.cloned.1.call-start = ((), (), s32[]{:S(2)}) async-start(), calls=%async_computation.27 | async-start | bytes 5971968 | tf_op jit(solution)/shard_map/reduce_scatter | solution.py:310
  538.1 417.6 %reduce-scatter.29.cloned.1.call-start = ((), (), s32[]{:S(2)}) async-start(), calls=%async_computation.25 | async-start | bytes 11943936 | tf_op jit(solution)/shard_map/reduce_scatter | solution.py:307
  557.0 25.9 %copy-start.50 = (f32[1152]{0:T(1024)S(1)}, f32[1152]{0:T(1024)}, u32[]{:S(2)}) copy-start(f32[1152]{0:T(1024)} %get-tuple-element.114) | copy-start | bytes 13828
  557.0 25.9 %copy-start.51 = (f32[1152]{0:T(1024)S(1)}, f32[1152]{0:T(1024)}, u32[]{:S(2)}) copy-start(f32[1152]{0:T(1024)} %get-tuple-element.116) | copy-start | bytes 13828
  557.0 25.9 %copy-start.79 = (f32[72]{0:T(128)S(1)}, f32[72]{0:T(128)}, u32[]{:S(2)}) copy-start(f32[72]{0:T(128)} %get-tuple-element.85) | copy-start | bytes 868
  557.0 25.9 %copy-start.80 = (f32[72]{0:T(128)S(1)}, f32[72]{0:T(128)}, u32[]{:S(2)}) copy-start(f32[72]{0:T(128)} %get-tuple-element.87) | copy-start | bytes 868
  (81 other events, 298.7 us)
Sparse Core Ops, SparseCore 0:
  9.6 71.6 all-gather.4
  98.7 46.4 reduce-scatter.12
  149.8 49.3 all-gather.6
  201.2 48.7 all-gather.8
  265.7 46.4 reduce-scatter.16
  314.4 47.0 reduce-scatter.14
  368.6 49.3 all-gather.10
  439.3 46.4 reduce-scatter.18
  489.3 64.7 reduce-scatter.24
  558.0 48.4 reduce-scatter.26
  610.5 39.2 reduce-scatter.22
  653.6 56.7 reduce-scatter.20
  714.2 36.6 reduce-scatter.30
  754.8 53.7 reduce-scatter.34
  812.5 56.8 reduce-scatter.32
  873.3 82.3 reduce-scatter.28
where the time goes:
time: 972 us; the launch traced here: 962 us
  waiting for transfers between devices  633 us (65%)
  blocking collectives  133 us (14%)
  matrix products  99 us (10%)
  other arithmetic  47.9 us (5%)
  local copies, waits for them, and re-layouts  30.4 us (3%)
  between operations  16.6 us (2%)
    reduce_scatter x1, waiting for transfers between devices, shards(): lax.psum_scatter(modulate_local, 'dp', scatter_dimension=0, tiled=True)  86.3 us
    reduce_scatter x1, waiting for transfers between devices, shards(): lax.psum_scatter(embed_local, 'dp', scatter_dimension=0, tiled=True)  60.7 us
    reduce_scatter x1, waiting for transfers between devices, shards(): lax.psum_scatter(project_grad, 'dp', scatter_dimension=0, tiled=True)  60.7 us
    reduce_scatter x1, waiting for transfers between devices, shards(): lax.psum_scatter(class_grad, 'dp', scatter_dimension=1, tiled=True)  57.7 us
    all_gather x1, waiting for transfers between devices, shards(): piece = lax.all_gather(attend_grad, 'tensor', axis=0, tiled=True)  49.5 us
    all_gather x1, waiting for transfers between devices, shards(): mod_two_all = lax.all_gather(mod_two, 'tensor', axis=0, tiled=True)  46.1 us
    reduce_scatter x1, waiting for transfers between devices, shards(): lax.psum_scatter(jnp.einsum('blf,fd->bld', piece, down_weight, preferred_...  44.8 us
    all_gather x1, blocking collectives, shards(): lax.all_gather(modulation_part, 'tensor', axis=2, tiled=True)  44.6 us
  transfers between devices with their start and end apart: 16, of which 15 were waited for; matrix products, arithmetic and copies ran while one was open for 11% of the time, Pallas kernels for 0%

commit v1 on v0

--- a/solution.py
+++ b/solution.py
@@ -149,7 +149,18 @@
     residual = token_local + attend_gate * attend_branch
     normed_two, inverse_two = layer_norm(residual)
     mod_two = (normed_two * (1.0 + feed_scale) + feed_shift).astype(jnp.bfloat16)
-    mod_two_all = lax.all_gather(mod_two, "tensor", axis=0, tiled=True)
+    r1 = jax.lax.axis_size("tensor")
+    even = jax.lax.axis_index("tensor")
+    long_array, e_now = (r1, even)
+    mod_two_all, r2 = (mod_two, 1)
+    while r2 < long_array:
+        out_arr = jax.lax.ppermute(
+            mod_two_all, axis_name="tensor", perm=[(t, t ^ r2) for t in range(long_array)]
+        )
+        piece_now = jnp.concatenate([mod_two_all, out_arr], axis=0)
+        y = jnp.concatenate([out_arr, mod_two_all], axis=0)
+        mod_two_all = jnp.where(e_now & r2 == 0, piece_now, y)
+        r2 = 2 * r2
     gate_up = jnp.einsum(
         "bld,dkf->blkf", mod_two_all, expand_weight, preferred_element_type=jnp.float32
     )

time: 972 us -> 982 us (1.010)
    ppermute x0 -> x2, waiting for transfers between devices: none -> 95.6 us  [shards(): jax.lax.ppermute(mod_two_all, axis_name='tensor', perm=[(t, t ^ r2) for t...]
    all_gather x1 -> x0, waiting for transfers between devices: 46.1 us -> none  [shards(): mod_two_all = lax.all_gather(mod_two, 'tensor', axis=0, tiled=True)]
    all_gather x1, waiting for transfers between devices: 41.2 us -> 0.01 us  [shards(): piece = lax.all_gather(branch_grad, 'tensor', axis=0, tiled=True)]
    unnamed x185 -> x187, local copies, waits for them, and re-layouts: 22.2 us -> 21.7 us
  transfers between devices with their start and end apart: 16 -> 17, of which waited for: 15 -> 15; matrix products, arithmetic and copies ran while one was open for 11% -> 12% of each run, Pallas kernels for 0% -> 0%
where the time goes in v1:
time: 982 us; the launch traced here: 972 us
  waiting for transfers between devices  637 us (65%)
  blocking collectives  133 us (14%)
  matrix products  101 us (10%)
  other arithmetic  50.7 us (5%)
  local copies, waits for them, and re-layouts  29.8 us (3%)
  between operations  16.7 us (2%)
    ppermute x2, waiting for transfers between devices, shards(): jax.lax.ppermute(mod_two_all, axis_name='tensor', perm=[(t, t ^ r2) for t...  95.6 us
    reduce_scatter x1, waiting for transfers between devices, shards(): lax.psum_scatter(modulate_local, 'dp', scatter_dimension=0, tiled=True)  86.3 us
    reduce_scatter x1, waiting for transfers between devices, shards(): lax.psum_scatter(project_grad, 'dp', scatter_dimension=0, tiled=True)  60.8 us
    reduce_scatter x1, waiting for transfers between devices, shards(): lax.psum_scatter(embed_local, 'dp', scatter_dimension=0, tiled=True)  60.7 us
    reduce_scatter x1, waiting for transfers between devices, shards(): lax.psum_scatter(class_grad, 'dp', scatter_dimension=1, tiled=True)  57.8 us
    all_gather x1, waiting for transfers between devices, shards(): piece = lax.all_gather(attend_grad, 'tensor', axis=0, tiled=True)  49.5 us
    reduce_scatter x1, waiting for transfers between devices, shards(): lax.psum_scatter(jnp.einsum('blf,fd->bld', piece, down_weight, preferred_...  44.8 us
    all_gather x1, blocking collectives, shards(): lax.all_gather(modulation_part, 'tensor', axis=2, tiled=True)  44.6 us
  transfers between devices with their start and end apart: 17, of which 15 were waited for; matrix products, arithmetic and copies ran while one was open for 12% of the time, Pallas kernels for 0%

profile of v1, /device:TPU:0, one launch (start us, length us, event | category | flops | bytes accessed | tf_op | source)
XLA Modules:
  0.0 972.3 jit_solution(3821256327253653584)
XLA Ops:
  23.0 44.6 %all_gather.12 = bf16[4,6,1152]{1,0,2:T(4,128)(2,1)} all-gather(bf16[4,6,288]{1,0,2:T(4,128)(2,1)S(1)} %copy.105), channel_id=1, replica_groups=mesh['dp'=8,'tensor'=4] {'tensor'}, dimensions={2}, use_global_device_ids=true | all-gather | bytes 69120 | tf_op jit(solution)/shard_map/all_gather | solution.py:110
  70.1 11.3 %all-gather.4.cloned.1.call-done = bf16[4,256,1152]{2,1,0:T(8,128)(2,1)} async-done(((bf16[1,256,1152]{2,1,0:T(8,128)(2,1)}), bf16[4,256,1152]{2,1,0:T(8,128)(2,1)}) %all-gather.4.cloned.1.call-update) | async-done | bytes 2359312 | tf_op jit(solution)/shard_map/all_gather | solution.py:109
  105.2 39.6 %reduce-scatter.13.cloned.1.call-done = bf16[1,256,1152]{2,1,0:T(8,128)(2,1)} async-done(((bf16[4,256,1152]{2,1,0:T(8,128)(2,1)}), bf16[1,256,1152]{2,1,0:T(8,128)(2,1)}) %reduce-scatter.13.cloned.1.call-update) | async-done | bytes 589840 | tf_op jit(solution)/shard_map/reduce_scatter | solution.py:139
  149.5 36.5 %collective-permute-done = bf16[1,256,1152]{2,1,0:T(8,128)(2,1)} collective-permute-done((bf16[1,256,1152]{2,1,0:T(8,128)(2,1)}, bf16[1,256,1152]{2,1,0:T(8,128)(2,1)}, u32[]{:S(2)}, u32[]{:S(2)}) %collective-permute-start) | collective-permute-done | bytes 589856 | tf_op jit(solution)/shard_map/ppermute | solution.py:157
  190.2 59.1 %collective-permute-done.1 = bf16[2,256,1152]{2,1,0:T(8,128)(2,1)} collective-permute-done((bf16[2,256,1152]{2,1,0:T(8,128)(2,1)}, bf16[2,256,1152]{2,1,0:T(8,128)(2,1)}, u32[]{:S(2)}, u32[]{:S(2)}) %collective-permute-start.1) | collective-permute-done | bytes 1179680 | tf_op jit(solution)/shard_map/ppermute | solution.py:157
  249.3 10.4 %fusion.7 = f32[4,256,2,768]{3,1,2,0:T(8,128)} fusion(bf16[1152,2,768]{2,1,0:T(2,128)(2,1)} %param.30, bf16[2,256,1152]{2,1,0:T(8,128)(2,1)} %collective-permute-done.1, bf16[2,256,1152]{2,1,0:T(8,128)(2,1)} %maximum_select_fusion.1, pred[]{:T(512)S(6)} %eq.24), kind=kOutput, calls=%fused_computation.22 | convolution fusion | flops 3634495488 | bytes 12189697 | tf_op jit(solution)/shard_map/bld,dkf->blkf/dot_general | solution.py:164
  259.7 8.4 fusion.30
  282.6 39.5 %reduce-scatter.17.cloned.1.call-done = bf16[1,256,1152]{2,1,0:T(8,128)(2,1)} async-done(((bf16[4,256,1152]{2,1,0:T(8,128)(2,1)}), bf16[1,256,1152]{2,1,0:T(8,128)(2,1)}) %reduce-scatter.17.cloned.1.call-update) | async-done | bytes 589840 | tf_op jit(solution)/shard_map/reduce_scatter | solution.py:195
  326.5 44.8 %reduce-scatter.15.cloned.1.call-done = bf16[1,256,1152]{2,1,0:T(8,128)(2,1)} async-done(((bf16[4,256,1152]{2,1,0:T(8,128)(2,1)}), bf16[1,256,1152]{2,1,0:T(8,128)(2,1)}) %reduce-scatter.15.cloned.1.call-update) | async-done | bytes 589840 | tf_op jit(solution)/shard_map/reduce_scatter | solution.py:171
  378.3 49.5 %all-gather.8.cloned.1.call-done = bf16[4,256,1152]{2,1,0:T(8,128)(2,1)} async-done(((bf16[1,256,1152]{2,1,0:T(8,128)(2,1)}), bf16[4,256,1152]{2,1,0:T(8,128)(2,1)}) %all-gather.8.cloned.1.call-update) | async-done | bytes 2359312 | tf_op jit(solution)/shard_map/all_gather | solution.py:208
  449.4 10.2 %convolution_bitcast_fusion = f32[1152,2,768]{2,0,1:T(8,128)} fusion(bf16[4,256,1,768]{3,1,0,2:T(8,128)(2,1)} %copy-done.89, bf16[4,256,1,768]{3,1,0,2:T(8,128)(2,1)} %copy-done.88, bf16[2,256,1152]{2,1,0:T(8,128)(2,1)} %collective-permute-done.1, bf16[2,256,1152]{2,1,0:T(8,128)(2,1)} %maximum_select_fusion.1, pred[]{:T(512)S(6)} %eq.24), kind=kOutput, calls=%fused_computation.5 | convolution fusion | flops 3640786944 | bytes 12582913 | tf_op jit(solution)/shard_map/bld,blkf->dkf/dot_general | solution.py:191
  471.0 8.1 convolution_bitcast_fusion.1
  480.0 15.6 %reduce-scatter.19.cloned.1.call-done = bf16[1,256,1152]{2,1,0:T(8,128)(2,1)} async-done(((bf16[4,256,1152]{2,1,0:T(8,128)(2,1)}), bf16[1,256,1152]{2,1,0:T(8,128)(2,1)}) %reduce-scatter.19.cloned.1.call-update) | async-done | bytes 589840 | tf_op jit(solution)/shard_map/reduce_scatter | solution.py:247
  508.3 8.8 all_to_all.4
  522.8 16.3 %psum.47 = f32[4,1152]{1,0:T(4,128)S(1)} all-reduce(f32[4,1152]{1,0:T(4,128)S(1)} %convolution_bitcast_fusion.4), channel_id=1, replica_groups=mesh['dp'=8,'tensor'=4] {'tensor'}, use_global_device_ids=true, to_apply=%region_42.43 | all-reduce | flops 4608 | bytes 36864 | tf_op jit(solution)/shard_map/psum | solution.py:277
  555.5 8.4 reduce-scatter.25.cloned.1.call-done
  568.2 22.9 %all-reduce.15 = (f32[1152]{0:T(1024)S(1)}, f32[1152]{0:T(1024)S(1)}) all-reduce(f32[1152]{0:T(1024)S(1)} %get-tuple-element.164, f32[1152]{0:T(1024)S(1)} %get-tuple-element.110), channel_id=12, replica_groups=mesh['dp'=8,'tensor'=4] {'dp'}, use_global_device_ids=true, to_apply=%region_45.46.clone | all-reduce | flops 2304 | bytes 18432
  592.8 40.8 %all-reduce.14 = (f32[72]{0:T(128)}, f32[72]{0:T(128)}, f32[1152]{0:T(1024)}, f32[1152]{0:T(1024)}, f32[6,1152]{1,0:T(8,128)}) all-reduce(f32[72]{0:T(128)S(1)} %copy-done.81, f32[72]{0:T(128)S(1)} %copy-done.80, f32[1152]{0:T(1024)S(1)} %copy-done.52, f32[1152]{0:T(1024)S(1)} %copy-done.51, ...), channel_id=1, replica_groups=mesh['dp'=8,'tensor'=4] {'dp','tensor'}, use_global_device_ids=true, to_apply=%region_23.24 | all-reduce | flops 9360 | bytes 74880 | tf_op jit(solution)/shard_map/psum | solution.py:288
  633.6 26.0 %reduce-scatter.23.cloned.1.call-done = f32[288,144]{0,1:T(8,128)} async-done(((f32[288,1152]{0,1:T(8,128)}), f32[288,144]{0,1:T(8,128)}) %reduce-scatter.23.cloned.1.call-update) | async-done | bytes 165904 | tf_op jit(solution)/shard_map/reduce_scatter | solution.py:314
  659.5 60.8 %reduce-scatter.21.cloned.1.call-done = f32[144,3,288]{2,0,1:T(8,128)} async-done(((f32[1152,3,288]{2,0,1:T(8,128)}), f32[144,3,288]{2,0,1:T(8,128)}) %reduce-scatter.21.cloned.1.call-update) | async-done | bytes 497680 | tf_op jit(solution)/shard_map/reduce_scatter | solution.py:313
  720.4 40.4 %reduce-scatter.31.cloned.1.call-done = f32[256,144]{0,1:T(8,128)} async-done(((f32[256,1152]{0,1:T(8,128)}), f32[256,144]{0,1:T(8,128)}) %reduce-scatter.31.cloned.1.call-update) | async-done | bytes 147472 | tf_op jit(solution)/shard_map/reduce_scatter | solution.py:319
  760.7 57.8 %reduce-scatter.35.cloned.1.call-done = f32[1000,144]{0,1:T(8,128)} async-done(((f32[1000,1152]{0,1:T(8,128)}), f32[1000,144]{0,1:T(8,128)}) %reduce-scatter.35.cloned.1.call-update) | async-done | bytes 576016 | tf_op jit(solution)/shard_map/reduce_scatter | solution.py:317
  818.6 60.7 %reduce-scatter.33.cloned.1.call-done = f32[144,1152]{1,0:T(8,128)} async-done(((f32[1152,1152]{1,0:T(8,128)}), f32[144,1152]{1,0:T(8,128)}) %reduce-scatter.33.cloned.1.call-update) | async-done | bytes 663568 | tf_op jit(solution)/shard_map/reduce_scatter | solution.py:321
  879.3 86.3 %reduce-scatter.29.cloned.1.call-done = f32[144,6,288]{2,0,1:T(8,128)} async-done(((f32[1152,6,288]{2,0,1:T(8,128)}), f32[144,6,288]{2,0,1:T(8,128)}) %reduce-scatter.29.cloned.1.call-update) | async-done | bytes 995344 | tf_op jit(solution)/shard_map/reduce_scatter | solution.py:318
  (326 shorter events, 148.8 us)
Async XLA Ops:
  7.2 74.1 %all-gather.4.cloned.1.call-start = ((), (), s32[]{:S(2)}) async-start(), calls=%async_computation.13 | async-start | bytes 2949120 | tf_op jit(solution)/shard_map/all_gather | solution.py:109
  7.9 136.8 %reduce-scatter.13.cloned.1.call-start = ((), (), s32[]{:S(2)}) async-start(), calls=%async_computation.14 | async-start | bytes 2949120 | tf_op jit(solution)/shard_map/reduce_scatter | solution.py:139
  8.7 79.8 %copy-start.71 = (f32[72]{0:T(128)}, f32[72]{0:T(128)S(1)}, u32[]{:S(2)}) copy-start(f32[72]{0:T(128)S(1)} %convert_element_type.252) | copy-start | bytes 868
  9.3 79.4 %copy-start.73 = (f32[72]{0:T(128)}, f32[72]{0:T(128)S(1)}, u32[]{:S(2)}) copy-start(f32[72]{0:T(128)S(1)} %convert_element_type.255) | copy-start | bytes 868
  98.2 46.6 %copy-start.3 = (bf16[1,256,1152]{2,1,0:T(8,128)(2,1)S(1)}, bf16[1,256,1152]{2,1,0:T(8,128)(2,1)}, u32[]{:S(2)}) copy-start(bf16[1,256,1152]{2,1,0:T(8,128)(2,1)} %param.20) | copy-start | bytes 1769476
  98.2 161.5 %all-gather.6.cloned.1.call-start = ((), (), s32[]{:S(2)}) async-start(), calls=%async_computation.16 | async-start | bytes 2949120 | tf_op jit(solution)/shard_map/all_gather | solution.py:183
  103.7 218.3 %reduce-scatter.17.cloned.1.call-start = ((), (), s32[]{:S(2)}) async-start(), calls=%async_computation.17 | async-start | bytes 2949120 | tf_op jit(solution)/shard_map/reduce_scatter | solution.py:195
  148.7 37.4 %collective-permute-start = (bf16[1,256,1152]{2,1,0:T(8,128)(2,1)}, bf16[1,256,1152]{2,1,0:T(8,128)(2,1)}, u32[]{:S(2)}, u32[]{:S(2)}) collective-permute-start(bf16[1,256,1152]{2,1,0:T(8,128)(2,1)} %add_convert_fusion), channel_id=1, source_target_pairs={{0,1},{1,0},{2,3},{3,2},{4,5},{5,4},{6,7},{7,6},{8,9},{9,8},{10,11... | collective-permute-start | bytes 1769480 | tf_op jit(solution)/shard_map/ppermute | solution.py:157
  188.9 60.4 %collective-permute-start.1 = (bf16[2,256,1152]{2,1,0:T(8,128)(2,1)}, bf16[2,256,1152]{2,1,0:T(8,128)(2,1)}, u32[]{:S(2)}, u32[]{:S(2)}) collective-permute-start(bf16[2,256,1152]{2,1,0:T(8,128)(2,1)} %maximum_select_fusion.1), channel_id=1, source_target_pairs={{0,2},{1,3},{2,0},{3,1},{4,6},{5,7},{6,4},{7,5},{8,10},{9,11},{10,... | collective-permute-start | bytes 3538952 | tf_op jit(solution)/shard_map/ppermute | solution.py:157
  275.3 96.0 %reduce-scatter.15.cloned.1.call-start = ((), (), s32[]{:S(2)}) async-start(), calls=%async_computation.15 | async-start | bytes 2949120 | tf_op jit(solution)/shard_map/reduce_scatter | solution.py:171
  281.0 146.7 %all-gather.8.cloned.1.call-start = ((), (), s32[]{:S(2)}) async-start(), calls=%async_computation.18 | async-start | bytes 2949120 | tf_op jit(solution)/shard_map/all_gather | solution.py:208
  378.2 117.3 %reduce-scatter.19.cloned.1.call-start = ((), (), s32[]{:S(2)}) async-start(), calls=%async_computation.19 | async-start | bytes 2949120 | tf_op jit(solution)/shard_map/reduce_scatter | solution.py:247
  448.9 115.0 %reduce-scatter.25.cloned.1.call-start = ((), (), s32[]{:S(2)}) async-start(), calls=%async_computation.22 | async-start | bytes 7962624 | tf_op jit(solution)/shard_map/reduce_scatter | solution.py:315
  459.6 174.0 %reduce-scatter.27.cloned.1.call-start = ((), (), s32[]{:S(2)}) async-start(), calls=%async_computation.23 | async-start | bytes 3981312 | tf_op jit(solution)/shard_map/reduce_scatter | solution.py:316
  465.7 193.9 %reduce-scatter.23.cloned.1.call-start = ((), (), s32[]{:S(2)}) async-start(), calls=%async_computation.21 | async-start | bytes 1990656 | tf_op jit(solution)/shard_map/reduce_scatter | solution.py:314
  470.3 250.0 %reduce-scatter.21.cloned.1.call-start = ((), (), s32[]{:S(2)}) async-start(), calls=%async_computation.20 | async-start | bytes 5971968 | tf_op jit(solution)/shard_map/reduce_scatter | solution.py:313
  479.3 281.5 %reduce-scatter.31.cloned.1.call-start = ((), (), s32[]{:S(2)}) async-start(), calls=%async_computation.25 | async-start | bytes 1327104 | tf_op jit(solution)/shard_map/reduce_scatter | solution.py:319
  541.4 277.1 %reduce-scatter.35.cloned.1.call-start = ((), (), s32[]{:S(2)}) async-start(), calls=%async_computation.27 | async-start | bytes 5308416 | tf_op jit(solution)/shard_map/reduce_scatter | solution.py:317
  544.4 334.8 %reduce-scatter.33.cloned.1.call-start = ((), (), s32[]{:S(2)}) async-start(), calls=%async_computation.26 | async-start | bytes 5971968 | tf_op jit(solution)/shard_map/reduce_scatter | solution.py:321
  547.8 417.8 %reduce-scatter.29.cloned.1.call-start = ((), (), s32[]{:S(2)}) async-start(), calls=%async_computation.24 | async-start | bytes 11943936 | tf_op jit(solution)/shard_map/reduce_scatter | solution.py:318
  566.8 25.9 %copy-start.51 = (f32[1152]{0:T(1024)S(1)}, f32[1152]{0:T(1024)}, u32[]{:S(2)}) copy-start(f32[1152]{0:T(1024)} %get-tuple-element.114) | copy-start | bytes 13828
  566.8 25.9 %copy-start.52 = (f32[1152]{0:T(1024)S(1)}, f32[1152]{0:T(1024)}, u32[]{:S(2)}) copy-start(f32[1152]{0:T(1024)} %get-tuple-element.116) | copy-start | bytes 13828
  566.8 25.9 %copy-start.80 = (f32[72]{0:T(128)S(1)}, f32[72]{0:T(128)}, u32[]{:S(2)}) copy-start(f32[72]{0:T(128)} %get-tuple-element.85) | copy-start | bytes 868
  566.8 25.9 %copy-start.81 = (f32[72]{0:T(128)S(1)}, f32[72]{0:T(128)}, u32[]{:S(2)}) copy-start(f32[72]{0:T(128)} %get-tuple-element.87) | copy-start | bytes 868
  (83 other events, 318.9 us)
Sparse Core Ops, SparseCore 0:
  9.6 71.7 all-gather.3
  98.3 46.4 reduce-scatter.12
  146.9 69.3 all-gather.5
  275.4 46.5 reduce-scatter.16
  324.2 47.0 reduce-scatter.14
  378.4 49.3 all-gather.7
  449.1 46.4 reduce-scatter.18
  499.1 64.7 reduce-scatter.24
  568.0 48.4 reduce-scatter.26
  620.2 39.2 reduce-scatter.22
  663.5 56.7 reduce-scatter.20
  724.0 36.6 reduce-scatter.30
  764.7 53.7 reduce-scatter.34
  822.4 56.8 reduce-scatter.32
  883.2 82.3 reduce-scatter.28
